TPU v7x, 8 devices: a whole 2x2x1 slice. The times are simulated.
8 devices in a mesh: col: 4 (over z, y, x), row: 2 (over core).
Axes of the slice: x: 2, y: 2, z: 1, core: 2. Of those that a mesh axis runs over, the one named last changes fastest.
Arguments:
- x_in: bfloat16 [1, 96, 768, 256], P(None, 'row', 'col')
- a_pre: bfloat16 [1, 96, 768, 256], P(None, 'row', 'col')
- g_out: bfloat16 [1, 96, 768, 256], P(None, 'row', 'col')
- w_one: bfloat16 [3, 3, 256, 256], replicated
- w_two: bfloat16 [3, 3, 256, 256], replicated
Outputs:
- output 1: bfloat16 [1, 96, 768, 256], P(None, 'row', 'col')
- output 2: float32 [3, 3, 256, 256], replicated
- output 3: float32 [3, 3, 256, 256], replicated
All inputs are finite; a program needn't handle non-finite values.
Results may differ from a plain program's by a relative error of at most 0.001.
Values are sent between devices in bfloat16 or wider.
A program may use at most 1 GiB of HBM per device.

v0:
```python
import jax
import jax.numpy as jnp
from jax import lax
from jax.sharding import PartitionSpec as P

DATA_DIMS = ("NHWC", "HWOI", "NHWC")


def gelu_slope(pre_act):
    tanh_scale = 0.7978845608028654
    cube_coef = 0.044715
    tanh_val = jnp.tanh(tanh_scale * (pre_act + cube_coef * pre_act * pre_act * pre_act))
    return 0.5 * (1.0 + tanh_val) + 0.5 * pre_act * (1.0 - tanh_val * tanh_val) * tanh_scale * (1.0 + 3.0 * cube_coef * pre_act * pre_act)


def conv_valid(lhs_arr, rhs_arr):
    return lax.conv_general_dilated(lhs_arr, rhs_arr, (1, 1), "VALID", dimension_numbers=DATA_DIMS, preferred_element_type=jnp.float32)


def tap_grads(tile_in, grad_wide):
    row_count = tile_in.shape[1]
    col_count = tile_in.shape[2]
    return jnp.stack([jnp.stack([jnp.einsum("bhwi,bhwo->io", tile_in, grad_wide[:, 2 - tap_row:2 - tap_row + row_count, 2 - tap_col:2 - tap_col + col_count], preferred_element_type=jnp.float32) for tap_col in range(3)]) for tap_row in range(3)])


def shift_pairs(count):
    forward_pairs = [(source, source + 1) for source in range(count - 1)]
    backward_pairs = [(source + 1, source) for source in range(count - 1)]
    return forward_pairs, backward_pairs


def solution(mesh):
    row_down, row_up = shift_pairs(mesh.shape["row"])
    col_down, col_up = shift_pairs(mesh.shape["col"])

    def add_halo(tile):
        from_above = lax.ppermute(tile[:, -1:], "row", row_down)
        from_below = lax.ppermute(tile[:, :1], "row", row_up)
        tall = jnp.concatenate([from_above, tile, from_below], axis=1)
        from_left = lax.ppermute(tall[:, :, -1:], "col", col_down)
        from_right = lax.ppermute(tall[:, :, :1], "col", col_up)
        return jnp.concatenate([from_left, tall, from_right], axis=2)

    def local_step(x_tile, a_tile, g_tile, w_one, w_two):
        a_val = a_tile.astype(jnp.float32)
        z_act = jax.nn.gelu(a_val, approximate=True).astype(jnp.bfloat16)
        g_wide = add_halo(g_tile)
        d_z = conv_valid(g_wide, w_two[::-1, ::-1])
        w2_part = tap_grads(z_act, g_wide)
        d_a = (d_z * gelu_slope(a_val)).astype(jnp.bfloat16)
        grad_wide = add_halo(d_a)
        d_x = (conv_valid(grad_wide, w_one[::-1, ::-1]) + g_tile.astype(jnp.float32)).astype(jnp.bfloat16)
        w1_part = tap_grads(x_tile, grad_wide)
        d_w1, d_w2 = lax.psum((w1_part, w2_part), ("row", "col"))
        return d_x, d_w1, d_w2

    tile_spec = P(None, "row", "col", None)
    return jax.shard_map(local_step, mesh=mesh, in_specs=(tile_spec, tile_spec, tile_spec, P(), P()), out_specs=(tile_spec, P(), P()), check_vma=False)
```

profile of v0, /device:TPU:0, one launch (start us, length us, event | category | flops | bytes accessed | tf_op | source)
XLA Modules:
  0.0 240.8 jit_solution(7173415646101468910)
XLA Ops:
  12.6 7.9 %fusion.146 = f32[1,256,256]{2,1,0:T(8,128)} fusion(bf16[1,48,192,256]{3,2,1,0:T(8,128)(2,1)} %param.7, bf16[1,48,192,256]{3,2,1,0:T(8,128)(2,1)} %param.6), kind=kOutput, calls=%fused_computation.140 | convolution fusion | flops 1231552512 | bytes 9699328 | tf_op jit(solution)/shard_map/bhwi,bhwo->io/dot_general | solution.py:23
  22.6 5.3 %collective-permute-start.2 = (bf16[1,50,1,256]{3,2,1,0:T(2,128)(2,1)S(1)}, bf16[1,50,1,256]{3,2,1,0:T(2,128)(2,1)S(1)}, u32[]{:S(2)}, u32[]{:S(2)}) collective-permute-start(bf16[1,50,1,256]{3,2,1,0:T(2,128)(2,1)S(1)} %get-tuple-element.15), channel_id=1, source_target_pairs={{0,2},{2,4},{4,6},{1,3},{3,5},{5,7}} | collective-permute-start | bytes 76808 | tf_op jit(solution)/shard_map/ppermute | solution.py:40
  27.9 3.8 %fusion.117 = f32[1,256,256]{2,1,0:T(8,128)S(1)} fusion(bf16[1,1,192,256]{3,2,1,0:T(8,128)(2,1)S(1)} %collective-permute-done.1, bf16[1,48,192,256]{3,2,1,0:T(8,128)(2,1)S(1)} %bitcast.266, bf16[1,48,192,256]{3,2,1,0:T(8,128)(2,1)S(1)} %bitcast.272), kind=kOutput, calls=%fused_computation.131 | convolution fusion | flops 1233911808 | bytes 9797632 | tf_op jit(solution)/shard_map/bhwi,bhwo->io/dot_general | solution.py:23
  31.7 3.8 %fusion.123 = f32[1,256,256]{2,1,0:T(8,128)S(1)} fusion(bf16[1,48,192,256]{3,2,1,0:T(8,128)(2,1)S(1)} %bitcast.266, bf16[1,1,192,256]{3,2,1,0:T(8,128)(2,1)S(1)} %collective-permute-done, bf16[1,48,192,256]{3,2,1,0:T(8,128)(2,1)S(1)} %bitcast.272), kind=kOutput, calls=%fused_computation.133 | convolution fusion | flops 1233911808 | bytes 9797632 | tf_op jit(solution)/shard_map/bhwi,bhwo->io/dot_general | solution.py:23
  41.5 15.2 %broadcast_select_fusion.1 = f32[48,8,25,256]{3,1,2,0:T(8,128)} fusion(pred[8,25]{0,1:T(8,128)(4,1)S(1)} %copy-done.7, bf16[3,3,256,256]{3,2,1,0:T(8,128)(2,1)S(1)} %copy-done, bf16[50,1,7,2,256]{4,2,3,0,1:T(8,128)(2,1)S(1)} %slice.118, bf16[50,1,8,25,256]{4,2,3,0,1:T(8,128)(2,1)S(1)} %copy.11), kind=kOutput, calls=%fused_computation.54 | convolution fusion | flops 11343667200 | bytes 16488648 | tf_op jit(solution)/shard_map/conv_general_dilated | solution.py:17
  56.8 7.0 %copy.12 = f32[48,8,25,256]{3,0,2,1:T(8,128)S(1)} copy(f32[48,8,25,256]{3,1,2,0:T(8,128)} %broadcast_select_fusion.1) | data formatting | bytes 19660800 | tf_op jit(solution)/shard_map/conv_general_dilated | solution.py:17
  63.7 4.5 %slice.119 = f32[48,1,192,256]{3,0,2,1:T(8,128)} slice(f32[48,1,200,256]{3,0,2,1:T(8,128)S(1)} %bitcast.261), slice={[0:48], [0:1], [0:192], [0:256]} | slice | bytes 18874368 | tf_op jit(solution)/shard_map/conv_general_dilated | solution.py:17
  68.2 11.6 %fusion.9 = bf16[1,48,192,256]{3,2,1,0:T(8,128)(2,1)S(1)} fusion(bf16[1,48,192,256]{3,2,1,0:T(8,128)(2,1)} %param.6, f32[48,1,192,256]{3,0,2,1:T(8,128)} %slice.119), kind=kLoop, calls=%fused_computation.21 | loop fusion | flops 47185920 | bytes 18874368 | tf_op jit(solution)/shard_map/convert_element_type | solution.py:50
  81.2 3.6 %collective-permute-start.4 = (bf16[1,1,192,256]{3,2,1,0:T(8,128)(2,1)S(1)}, bf16[1,1,192,256]{3,2,1,0:T(8,128)(2,1)S(1)}, u32[]{:S(2)}, u32[]{:S(2)}) collective-permute-start(bf16[1,1,192,256]{3,2,1,0:T(8,128)(2,1)S(1)} %get-tuple-element.17), channel_id=1, source_target_pairs={{0,1},{2,3},{4,5},{6,7}} | collective-permute-start | bytes 294920 | tf_op jit(solution)/shard_map/ppermute | solution.py:37
  86.3 4.7 %fusion.120 = f32[1,256,256]{2,1,0:T(8,128)S(1)} fusion(bf16[1,50,1,256]{3,2,1,0:T(2,128)(2,1)S(1)} %collective-permute-done.3, bf16[1,50,192,256]{3,2,1,0:T(8,128)(2,1)S(1)} %bitcast.270, bf16[1,48,192,256]{3,2,1,0:T(8,128)(2,1)S(1)} %bitcast.274), kind=kOutput, calls=%fused_computation.132 | convolution fusion | flops 1240989696 | bytes 9921536 | tf_op jit(solution)/shard_map/bhwi,bhwo->io/dot_general | solution.py:23
  91.0 4.7 %fusion.126 = f32[1,256,256]{2,1,0:T(8,128)S(1)} fusion(bf16[1,50,192,256]{3,2,1,0:T(8,128)(2,1)S(1)} %bitcast.270, bf16[1,50,1,256]{3,2,1,0:T(2,128)(2,1)S(1)} %collective-permute-done.2, bf16[1,48,192,256]{3,2,1,0:T(8,128)(2,1)S(1)} %bitcast.274), kind=kOutput, calls=%fused_computation.134 | convolution fusion | flops 1240989696 | bytes 9921536 | tf_op jit(solution)/shard_map/bhwi,bhwo->io/dot_general | solution.py:23
  95.8 4.9 %fusion.129 = f32[1,256,256]{2,1,0:T(8,128)S(1)} fusion(bf16[1,50,1,256]{3,2,1,0:T(2,128)(2,1)S(1)} %collective-permute-done.3, bf16[1,50,192,256]{3,2,1,0:T(8,128)(2,1)S(1)} %bitcast.270, bf16[1,48,192,256]{3,2,1,0:T(8,128)(2,1)S(1)} %bitcast.274), kind=kOutput, calls=%fused_computation.135 | convolution fusion | flops 1240989696 | bytes 9921536 | tf_op jit(solution)/shard_map/bhwi,bhwo->io/dot_general | solution.py:23
  100.7 4.7 %fusion.132 = f32[1,256,256]{2,1,0:T(8,128)S(1)} fusion(bf16[1,50,1,256]{3,2,1,0:T(2,128)(2,1)S(1)} %collective-permute-done.3, bf16[1,50,192,256]{3,2,1,0:T(8,128)(2,1)S(1)} %bitcast.270, bf16[1,48,192,256]{3,2,1,0:T(8,128)(2,1)S(1)} %bitcast.274), kind=kOutput, calls=%fused_computation.136 | convolution fusion | flops 1240989696 | bytes 9921536 | tf_op jit(solution)/shard_map/bhwi,bhwo->io/dot_general | solution.py:23
  105.5 5.1 %fusion.135 = f32[1,256,256]{2,1,0:T(8,128)S(1)} fusion(bf16[1,50,1,256]{3,2,1,0:T(2,128)(2,1)S(1)} %collective-permute-done.2, bf16[1,50,192,256]{3,2,1,0:T(8,128)(2,1)S(1)} %bitcast.270, bf16[1,48,192,256]{3,2,1,0:T(8,128)(2,1)S(1)} %bitcast.274), kind=kOutput, calls=%fused_computation.137 | convolution fusion | flops 1240989696 | bytes 9921536 | tf_op jit(solution)/shard_map/bhwi,bhwo->io/dot_general | solution.py:23
  110.6 4.7 %fusion.138 = f32[1,256,256]{2,1,0:T(8,128)S(1)} fusion(bf16[1,50,1,256]{3,2,1,0:T(2,128)(2,1)S(1)} %collective-permute-done.2, bf16[1,50,192,256]{3,2,1,0:T(8,128)(2,1)S(1)} %bitcast.270, bf16[1,48,192,256]{3,2,1,0:T(8,128)(2,1)S(1)} %bitcast.274), kind=kOutput, calls=%fused_computation.138 | convolution fusion | flops 1240989696 | bytes 9921536 | tf_op jit(solution)/shard_map/bhwi,bhwo->io/dot_general | solution.py:23
  117.1 4.6 %collective-permute-start.6 = (bf16[1,50,1,256]{3,2,1,0:T(2,128)(2,1)S(1)}, bf16[1,50,1,256]{3,2,1,0:T(2,128)(2,1)S(1)}, u32[]{:S(2)}, u32[]{:S(2)}) collective-permute-start(bf16[1,50,1,256]{3,2,1,0:T(2,128)(2,1)S(1)} %get-tuple-element.13), channel_id=1, source_target_pairs={{0,2},{2,4},{4,6},{1,3},{3,5},{5,7}} | collective-permute-start | bytes 76808 | tf_op jit(solution)/shard_map/ppermute | solution.py:40
  127.7 5.2 %pad_maximum_fusion = (bf16[1,50,193,256]{3,2,1,0:T(8,128)(2,1)S(1)}, bf16[1,50,193,256]{3,2,1,0:T(8,128)(2,1)S(1)}) fusion(bf16[1,50,1,256]{3,2,1,0:T(2,128)(2,1)S(1)} %collective-permute-done.7, bf16[1,1,192,256]{3,2,1,0:T(8,128)(2,1)S(1)} %collective-permute-done.5, bf16[1,48,192,256]{3,2,1,0:T(8,128)(2,1)S(1)} %fusion.9, ...), kind=kLoop, calls=%fused_computation.51 | loop fusion | flops 39526400 | bytes 14848000 | tf_op jit(solution)/shard_map/concatenate | solution.py:42
  141.6 5.2 %maximum_bitcast_fusion.1 = bf16[50,1,194,256]{3,2,0,1:T(8,128)(2,1)S(1)} fusion(bf16[1,50,1,256]{3,2,1,0:T(2,128)(2,1)S(1)} %collective-permute-done.7, bf16[1,1,192,256]{3,2,1,0:T(8,128)(2,1)S(1)} %collective-permute-done.5, bf16[1,48,192,256]{3,2,1,0:T(8,128)(2,1)S(1)} %fusion.9, bf16[1,1,192,256]{3,2,1,0:T(8,128)(2,1)S(1)} %collective-permute-done.4, ...), kind=kLoop, calls=%fused_computation.50 | loop fusion | flops 24832000 | bytes 9932800 | tf_op jit(solution)/shard_map/concatenate | solution.py:42
  153.8 16.1 %broadcast_select_fusion = f32[48,8,25,256]{3,1,2,0:T(8,128)} fusion(pred[8,25]{0,1:T(8,128)(4,1)S(1)} %copy-done.8, bf16[3,3,256,256]{3,2,1,0:T(8,128)(2,1)S(1)} %copy-done.6, bf16[50,1,7,2,256]{4,2,3,0,1:T(8,128)(2,1)S(1)} %slice.122, bf16[50,1,8,25,256]{4,2,3,0,1:T(8,128)(2,1)} %copy-done.2), kind=kOutput, calls=%fused_computation.53 | convolution fusion | flops 11343667200 | bytes 16488648 | tf_op jit(solution)/shard_map/conv_general_dilated | solution.py:17
  169.8 7.0 %copy.17 = f32[48,8,25,256]{3,0,2,1:T(8,128)S(1)} copy(f32[48,8,25,256]{3,1,2,0:T(8,128)} %broadcast_select_fusion) | data formatting | bytes 19660800 | tf_op jit(solution)/shard_map/conv_general_dilated | solution.py:17
  176.8 8.1 %fusion.18 = bf16[1,48,192,256]{3,1,2,0:T(8,128)(2,1)} fusion(f32[48,1,200,256]{3,0,2,1:T(8,128)S(1)} %bitcast.262, bf16[1,48,192,256]{3,2,1,0:T(8,128)(2,1)} %param.7), kind=kLoop, calls=%fused_computation.31 | loop fusion | flops 7077888 | bytes 18874368 | tf_op jit(solution)/shard_map/convert_element_type | solution.py:52
  184.8 6.3 %copy.19 = bf16[1,48,192,256]{3,2,1,0:T(8,128)(2,1)} copy(bf16[1,48,192,256]{3,1,2,0:T(8,128)(2,1)} %fusion.18) | data formatting | bytes 9437184
  191.1 37.9 %all-reduce.3.cloned.1.call-done = (f32[3,3,256,256]{2,3,1,0:T(8,128)}, f32[3,3,256,256]{3,2,1,0:T(8,128)}) async-done(((f32[3,3,256,256]{2,3,1,0:T(8,128)}, f32[3,3,256,256]{3,2,1,0:T(8,128)}), (f32[3,3,256,256]{2,3,1,0:T(8,128)}, f32[3,3,256,256]{3,2,1,0:T(8,128)})) %all-reduce.3.cloned.1.call-update) | async-done | bytes 4718608 | tf_op jit(solution)/shard_map/psum | solution.py:54
  229.1 3.2 %copy.20 = f32[3,3,256,256]{3,2,1,0:T(8,128)} copy(f32[3,3,256,256]{2,3,1,0:T(8,128)} %get-tuple-element.9) | data formatting | bytes 4718592
  (90 shorter events, 40.9 us)
Async XLA Ops:
  7.2 34.3 %copy-start = (bf16[3,3,256,256]{3,2,1,0:T(8,128)(2,1)S(1)}, bf16[3,3,256,256]{3,2,1,0:T(8,128)(2,1)}, u32[]{:S(2)}) copy-start(bf16[3,3,256,256]{3,2,1,0:T(8,128)(2,1)} %param.9) | copy-start | bytes 3538948
  7.2 221.9 %all-reduce.3.cloned.1.call-start = ((), (), s32[]{:S(2)}) async-start(), calls=%async_computation | async-start | bytes 9437184 | tf_op jit(solution)/shard_map/psum | solution.py:54
  8.3 12.2 %collective-permute-start = (bf16[1,1,192,256]{3,2,1,0:T(8,128)(2,1)S(1)}, bf16[1,1,192,256]{3,2,1,0:T(8,128)(2,1)S(1)}, u32[]{:S(2)}, u32[]{:S(2)}) collective-permute-start(bf16[1,1,192,256]{3,2,1,0:T(8,128)(2,1)S(1)} %get-tuple-element.20), channel_id=1, source_target_pairs={{0,1},{2,3},{4,5},{6,7}} | collective-permute-start | bytes 294920 | tf_op jit(solution)/shard_map/ppermute | solution.py:37
  11.0 9.5 %slice-start = ((s8[4718592]{0:T(1024)(128)(4,1)}), s8[4194304]{0:T(1024)(128)(4,1)S(1)}, s32[]{:S(2)}) async-start(s8[4718592]{0:T(1024)(128)(4,1)} %bitcast.265), calls=%async_computation.1 | async-start | bytes 8388608
  11.1 9.5 %slice-start.1 = ((s8[4718592]{0:T(1024)(128)(4,1)}), s8[524288]{0:T(1024)(128)(4,1)S(1)}, s32[]{:S(2)}) async-start(s8[4718592]{0:T(1024)(128)(4,1)} %bitcast.265), calls=%async_computation.2 | async-start | bytes 1048576
  11.1 9.8 %collective-permute-start.1 = (bf16[1,1,192,256]{3,2,1,0:T(8,128)(2,1)S(1)}, bf16[1,1,192,256]{3,2,1,0:T(8,128)(2,1)S(1)}, u32[]{:S(2)}, u32[]{:S(2)}) collective-permute-start(bf16[1,1,192,256]{3,2,1,0:T(8,128)(2,1)S(1)} %get-tuple-element.19), channel_id=1, source_target_pairs={{1,0},{3,2},{5,4},{7,6}} | collective-permute-start | bytes 294920 | tf_op jit(solution)/shard_map/ppermute | solution.py:38
  20.5 7.4 %slice-start.6 = ((s8[4718592]{0:T(1024)(128)(4,1)}), s8[4194304]{0:T(1024)(128)(4,1)S(1)}, s32[]{:S(2)}) async-start(s8[4718592]{0:T(1024)(128)(4,1)} %bitcast.271), calls=%async_computation.7 | async-start | bytes 8388608
  20.5 7.3 %slice-start.7 = ((s8[4718592]{0:T(1024)(128)(4,1)}), s8[524288]{0:T(1024)(128)(4,1)S(1)}, s32[]{:S(2)}) async-start(s8[4718592]{0:T(1024)(128)(4,1)} %bitcast.271), calls=%async_computation.8 | async-start | bytes 1048576
  20.9 14.7 %copy-start.3 = (bf16[1,50,192,256]{3,2,1,0:T(8,128)(2,1)}, bf16[1,50,192,256]{3,2,1,0:T(8,128)(2,1)S(1)}, u32[]{:S(2)}) copy-start(bf16[1,50,192,256]{3,2,1,0:T(8,128)(2,1)S(1)} %constant_dynamic-update-slice_fusion) | copy-start | bytes 14745604
  21.0 14.6 %collective-permute-start.3 = (bf16[1,50,1,256]{3,2,1,0:T(2,128)(2,1)S(1)}, bf16[1,50,1,256]{3,2,1,0:T(2,128)(2,1)S(1)}, u32[]{:S(2)}, u32[]{:S(2)}) collective-permute-start(bf16[1,50,1,256]{3,2,1,0:T(2,128)(2,1)S(1)} %get-tuple-element.16), channel_id=1, source_target_pairs={{2,0},{4,2},{6,4},{3,1},{5,3},{7,5}} | collective-permute-start | bytes 76808 | tf_op jit(solution)/shard_map/ppermute | solution.py:41
  22.6 13.0 %collective-permute-start.2 = (bf16[1,50,1,256]{3,2,1,0:T(2,128)(2,1)S(1)}, bf16[1,50,1,256]{3,2,1,0:T(2,128)(2,1)S(1)}, u32[]{:S(2)}, u32[]{:S(2)}) collective-permute-start(bf16[1,50,1,256]{3,2,1,0:T(2,128)(2,1)S(1)} %get-tuple-element.15), channel_id=1, source_target_pairs={{0,2},{2,4},{4,6},{1,3},{3,5},{5,7}} | collective-permute-start | bytes 76808 | tf_op jit(solution)/shard_map/ppermute | solution.py:40
  63.7 21.1 %slice-start.2 = ((s8[4718592]{0:T(1024)(128)(4,1)}), s8[524288]{0:T(1024)(128)(4,1)S(1)}, s32[]{:S(2)}) async-start(s8[4718592]{0:T(1024)(128)(4,1)} %bitcast.267), calls=%async_computation.3 | async-start | bytes 1048576
  68.2 16.6 %slice-start.3 = ((s8[4718592]{0:T(1024)(128)(4,1)}), s8[4194304]{0:T(1024)(128)(4,1)S(1)}, s32[]{:S(2)}) async-start(s8[4718592]{0:T(1024)(128)(4,1)} %bitcast.267), calls=%async_computation.4 | async-start | bytes 8388608
  79.8 37.2 %collective-permute-start.5 = (bf16[1,1,192,256]{3,2,1,0:T(8,128)(2,1)S(1)}, bf16[1,1,192,256]{3,2,1,0:T(8,128)(2,1)S(1)}, u32[]{:S(2)}, u32[]{:S(2)}) collective-permute-start(bf16[1,1,192,256]{3,2,1,0:T(8,128)(2,1)S(1)} %get-tuple-element.18), channel_id=1, source_target_pairs={{1,0},{3,2},{5,4},{7,6}} | collective-permute-start | bytes 294920 | tf_op jit(solution)/shard_map/ppermute | solution.py:38
  81.1 5.1 %slice-start.4 = ((s8[4915200]{0:T(1024)(128)(4,1)}), s8[4194304]{0:T(1024)(128)(4,1)S(1)}, s32[]{:S(2)}) async-start(s8[4915200]{0:T(1024)(128)(4,1)} %bitcast.269), calls=%async_computation.5 | async-start | bytes 8388608
  81.1 5.1 %slice-start.8 = ((s8[4718592]{0:T(1024)(128)(4,1)}), s8[4194304]{0:T(1024)(128)(4,1)S(1)}, s32[]{:S(2)}) async-start(s8[4718592]{0:T(1024)(128)(4,1)} %bitcast.273), calls=%async_computation.9 | async-start | bytes 8388608
  81.1 5.1 %slice-start.5 = ((s8[4915200]{0:T(1024)(128)(4,1)}), s8[720896]{0:T(1024)(128)(4,1)S(1)}, s32[]{:S(2)}) async-start(s8[4915200]{0:T(1024)(128)(4,1)} %bitcast.269), calls=%async_computation.6 | async-start | bytes 1441792
  81.1 5.1 %slice-start.9 = ((s8[4718592]{0:T(1024)(128)(4,1)}), s8[524288]{0:T(1024)(128)(4,1)S(1)}, s32[]{:S(2)}) async-start(s8[4718592]{0:T(1024)(128)(4,1)} %bitcast.273), calls=%async_computation.10 | async-start | bytes 1048576
  81.2 35.9 %collective-permute-start.4 = (bf16[1,1,192,256]{3,2,1,0:T(8,128)(2,1)S(1)}, bf16[1,1,192,256]{3,2,1,0:T(8,128)(2,1)S(1)}, u32[]{:S(2)}, u32[]{:S(2)}) collective-permute-start(bf16[1,1,192,256]{3,2,1,0:T(8,128)(2,1)S(1)} %get-tuple-element.17), channel_id=1, source_target_pairs={{0,1},{2,3},{4,5},{6,7}} | collective-permute-start | bytes 294920 | tf_op jit(solution)/shard_map/ppermute | solution.py:37
  110.6 4.7 %copy-start.5 = (f32[1,256,256]{2,1,0:T(8,128)S(1)}, f32[1,256,256]{2,1,0:T(8,128)}, u32[]{:S(2)}) copy-start(f32[1,256,256]{2,1,0:T(8,128)} %fusion.146) | copy-start | bytes 786436
  117.1 9.0 %collective-permute-start.6 = (bf16[1,50,1,256]{3,2,1,0:T(2,128)(2,1)S(1)}, bf16[1,50,1,256]{3,2,1,0:T(2,128)(2,1)S(1)}, u32[]{:S(2)}, u32[]{:S(2)}) collective-permute-start(bf16[1,50,1,256]{3,2,1,0:T(2,128)(2,1)S(1)} %get-tuple-element.13), channel_id=1, source_target_pairs={{0,2},{2,4},{4,6},{1,3},{3,5},{5,7}} | collective-permute-start | bytes 76808 | tf_op jit(solution)/shard_map/ppermute | solution.py:40
  121.7 6.0 %collective-permute-start.7 = (bf16[1,50,1,256]{3,2,1,0:T(2,128)(2,1)S(1)}, bf16[1,50,1,256]{3,2,1,0:T(2,128)(2,1)S(1)}, u32[]{:S(2)}, u32[]{:S(2)}) collective-permute-start(bf16[1,50,1,256]{3,2,1,0:T(2,128)(2,1)S(1)} %get-tuple-element.14), channel_id=1, source_target_pairs={{2,0},{4,2},{6,4},{3,1},{5,3},{7,5}} | collective-permute-start | bytes 76808 | tf_op jit(solution)/shard_map/ppermute | solution.py:41
  184.8 48.8 %copy-start.1 = (bf16[3,3,256,256]{3,2,1,0:T(8,128)(2,1)S(1)}, bf16[3,3,256,256]{3,2,1,0:T(8,128)(2,1)}, u32[]{:S(2)}) copy-start(bf16[3,3,256,256]{3,2,1,0:T(8,128)(2,1)} %param.9) | copy-start | bytes 3538948
  229.1 3.2 %copy-start.4 = (f32[3,3,256,256]{3,2,1,0:T(8,128)S(1)}, f32[3,3,256,256]{3,2,1,0:T(8,128)}, u32[]{:S(2)}) copy-start(f32[3,3,256,256]{3,2,1,0:T(8,128)} %get-tuple-element.27) | copy-start | bytes 7077892
  (4 other events, 6.9 us)
Sparse Core Ops, SparseCore 0:
  153.8 75.2 all-reduce.2
where the time goes:
time: 245 us; the launch traced here: 241 us
  matrix products  89.1 us (36%)
  waiting for transfers between devices  39.5 us (16%)
  local copies, waits for them, and re-layouts  38.6 us (16%)
  other arithmetic  36.8 us (15%)
  starting transfers between devices  22 us (9%)
  between operations  14.9 us (6%)
    dot_general x18, matrix products, tap_grads(): jnp.einsum('bhwi,bhwo->io', tile_in, grad_wide[:, 2 - tap_row:2 - tap_row...  57.7 us
    psum x1, waiting for transfers between devices, local_step(): d_w1, d_w2 = lax.psum((w1_part, w2_part), ('row', 'col'))  37.9 us
    conv_general_dilated x2, matrix products, conv_valid(): lax.conv_general_dilated(lhs_arr, rhs_arr, (1, 1), 'VALID', dimension_num...  31.3 us
    conv_general_dilated x7, local copies, waits for them, and re-layouts, conv_valid(): lax.conv_general_dilated(lhs_arr, rhs_arr, (1, 1), 'VALID', dimension_num...  20.7 us
    unnamed x45, local copies, waits for them, and re-layouts  15.9 us
    concatenate x3, other arithmetic, add_halo(): return jnp.concatenate([from_left, tall, from_right], axis=2)  13.5 us
    convert_element_type x1, other arithmetic, local_step(): d_a = (d_z * gelu_slope(a_val)).astype(jnp.bfloat16)  11.6 us
    ppermute x2, starting transfers between devices, add_halo(): from_left = lax.ppermute(tall[:, :, -1:], 'col', col_down)  9.85 us
  transfers between devices with their start and end apart: 9, of which 2 were waited for; matrix products, arithmetic and copies ran while one was open for 37% of the time, Pallas kernels for 0%

commit v1 on v0

v1 whole, which is shorter than its diff:
```python
import functools

import jax
import jax.numpy as jnp
from jax import lax
from jax.experimental import pallas as pl
from jax.experimental.pallas import tpu as pltpu
from jax.sharding import PartitionSpec as P

MESH = pl.DeviceIdType.MESH
F32 = jnp.float32
BF16 = jnp.bfloat16
CH = 256
ROWS = 48
COLS = 192
PIX = ROWS * COLS
STEP = 4
SPAN = STEP * COLS
CHUNKS = ROWS // STEP
TAPS = 9
BASE_ONE = TAPS + CHUNKS
LAST_TICK = 2 * (TAPS + CHUNKS)
LAGS = (0, 2, 4, 6, 8, 10)


def gelu_slope(pre_act):
    tanh_scale = 0.7978845608028654
    cube_coef = 0.044715
    tanh_val = jnp.tanh(tanh_scale * (pre_act + cube_coef * pre_act * pre_act * pre_act))
    return 0.5 * (1.0 + tanh_val) + 0.5 * pre_act * (1.0 - tanh_val * tanh_val) * tanh_scale * (1.0 + 3.0 * cube_coef * pre_act * pre_act)


def kernel(n_row, n_col, x_hbm, a_hbm, g_hbm, w1_hbm, w2_hbm, dx_hbm, dw1_hbm, dw2_hbm,
           g0, g1, g2, d0, d1, d2, zt, xt, av, w1, w2, acc, res, r0, r1, r2, dza, dzb,
           lhg, rhg, lhd, rhd, clg, crg, cld, crd,
           in_sem, out_sem, dw_sem, hs_sem, hr_sem, as_sem, ar_sem):
    row = lax.axis_index("row")
    col = lax.axis_index("col")
    bx = lax.rem(col, 2)
    by = lax.div(col, 2)
    other = 1 - row
    col_x = col + 1 - 2 * bx
    col_y = col + 2 - 4 * by
    has_left = col > 0
    has_right = col < n_col - 1

    a_copies = [pltpu.make_async_copy(a_hbm.at[pl.ds(12 * q, 12)], av.at[pl.ds(12 * q, 12)], in_sem.at[q]) for q in range(4)]
    g_copy = pltpu.make_async_copy(g_hbm, g1.at[pl.ds(1, ROWS)], in_sem.at[4])
    x_copy = pltpu.make_async_copy(x_hbm, d1.at[pl.ds(1, ROWS)], in_sem.at[5])
    w2_copy = pltpu.make_async_copy(w2_hbm, w2, in_sem.at[6])
    w1_copy = pltpu.make_async_copy(w1_hbm, w1, in_sem.at[7])
    a_copies[0].start()
    g_copy.start()
    for q in range(1, 4):
        a_copies[q].start()
    x_copy.start()
    w2_copy.start()
    w1_copy.start()

    for buf in (lhg, rhg, lhd, rhd):
        buf[...] = jnp.zeros_like(buf)
    for buf in (g1, d1):
        buf[0] = jnp.zeros((COLS, CH), BF16)
        buf[ROWS + 1] = jnp.zeros((COLS, CH), BF16)

    barrier = pltpu.get_barrier_semaphore()
    for dc in range(n_col):
        for dr in range(n_row):
            if dc or dr:
                pl.semaphore_signal(barrier, inc=1, device_id={"col": lax.rem(col + dc, n_col), "row": lax.rem(row + dr, n_row)}, device_id_type=MESH)
    pl.semaphore_wait(barrier, n_col * n_row - 1)

    def frame_copies(which, plane, cl, cr, lh, rh):
        def remote(src, dst, k, dev):
            return pltpu.make_async_remote_copy(src_ref=src, dst_ref=dst, send_sem=hs_sem.at[which, k], recv_sem=hr_sem.at[which, k], device_id=dev, device_id_type=MESH)

        left = jnp.maximum(col - 1, 0)
        right = jnp.minimum(col + 1, n_col - 1)
        src8 = pl.multiple_of(40 * other, 8)
        dst8 = pl.multiple_of(56 * row, 8)
        pair = remote(plane.at[ROWS - (ROWS - 1) * row], plane.at[(ROWS + 1) * row], 0, {"col": col, "row": other})
        to_left = [remote(cl, rh.at[pl.ds(8, ROWS)], 1, {"col": left, "row": row}), remote(cl.at[pl.ds(src8, 8)], rh.at[pl.ds(dst8, 8)], 2, {"col": left, "row": other})]
        to_right = [remote(cr, lh.at[pl.ds(8, ROWS)], 3, {"col": right, "row": row}), remote(cr.at[pl.ds(src8, 8)], lh.at[pl.ds(dst8, 8)], 4, {"col": right, "row": other})]
        return pair, to_left, to_right

    def frame_send(copies):
        pair, to_left, to_right = copies
        pair.start()

        @pl.when(has_left)
        def _():
            for c in to_left:
                c.start()

        @pl.when(has_right)
        def _():
            for c in to_right:
                c.start()

    def frame_wait(copies):
        pair, to_left, to_right = copies
        pair.wait_recv()

        @pl.when(has_right)
        def _():
            for c in to_left:
                c.wait_recv()

        @pl.when(has_left)
        def _():
            for c in to_right:
                c.wait_recv()

    def frame_done(copies):
        pair, to_left, to_right = copies
        pair.wait_send()

        @pl.when(has_left)
        def _():
            for c in to_left:
                c.wait_send()

        @pl.when(has_right)
        def _():
            for c in to_right:
                c.wait_send()

    def unit_copies(u, j):
        half = 128 * row
        p_base, q_base = half, half + 64
        p_mine, q_mine = p_base + 32 * bx, q_base + 32 * by
        p_last, q_last = p_mine + 16 * by, q_mine + 16 * bx

        def rows(ref, start, size):
            return ref.at[u, pl.ds(pl.multiple_of(start, 16), size)]

        def remote(src, dst, k, dev):
            return pltpu.make_async_remote_copy(src_ref=src, dst_ref=dst, send_sem=as_sem.at[u, k], recv_sem=ar_sem.at[u, k], device_id=dev, device_id_type=MESH)

        core = {"col": col, "row": other}
        dev_x = {"col": col_x, "row": row}
        dev_y = {"col": col_y, "row": row}
        if j == 0:
            return [remote(rows(acc, 128 * other, 128), r0.at[u], 0, core)]
        if j == 1:
            return [remote(rows(acc, p_base + 32 * (1 - bx), 32), rows(r1, 0, 32), 1, dev_x), remote(rows(acc, q_base + 32 * (1 - by), 32), rows(r1, 32, 32), 2, dev_y)]
        if j == 2:
            return [remote(rows(acc, p_mine + 16 * (1 - by), 16), rows(r2, 0, 16), 3, dev_y), remote(rows(acc, q_mine + 16 * (1 - bx), 16), rows(r2, 16, 16), 4, dev_x)]
        if j == 3:
            return [remote(rows(res, p_last, 16), rows(res, p_last, 16), 5, dev_y), remote(rows(res, q_last, 16), rows(res, q_last, 16), 6, dev_x)]
        if j == 4:
            return [remote(rows(res, p_mine, 32), rows(res, p_mine, 32), 7, dev_x), remote(rows(res, q_mine, 32), rows(res, q_mine, 32), 8, dev_y)]
        return [remote(rows(res, half, 128), rows(res, half, 128), 9, core)]

    def add_rows(dst, u, start, size, src, src_start):
        at = pl.ds(pl.multiple_of(start, 16), size)
        dst[u, at, :] = acc[u, at, :] + src[u, pl.ds(src_start, size), :]

    def tap_of(v):
        tap_row = jnp.where(v < 1, 1, jnp.where(v < 3, 2 * (v - 1), lax.rem(v, 3)))
        tap_col = jnp.where(v < 3, 1, jnp.where(v < 6, 0, 2))
        return 3 * tap_row + tap_col

    def result_copy(u, first):
        if first:
            return pltpu.make_async_copy(res.at[u], dw2_hbm.at[tap_of(u)], dw_sem.at[u])
        return pltpu.make_async_copy(res.at[u], dw1_hbm.at[tap_of(u - TAPS)], dw_sem.at[u])

    def stage(u, j):
        for c in unit_copies(u, j - 1):
            c.wait_recv()
        half = 128 * row
        if j == 1:
            add_rows(acc, u, half, 128, r0, 0)
        elif j == 2:
            add_rows(acc, u, half + 32 * bx, 32, r1, 0)
            add_rows(acc, u, half + 64 + 32 * by, 32, r1, 32)
        elif j == 3:
            add_rows(res, u, half + 32 * bx + 16 * by, 16, r2, 0)
            add_rows(res, u, half + 64 + 32 * by + 16 * bx, 16, r2, 16)
        if j < 6:
            for c in unit_copies(u, j):
                c.start()
        else:
            for k in range(6):
                for c in unit_copies(u, k):
                    c.wait_send()

            @pl.when(u < TAPS)
            def _():
                result_copy(u, True).start()

            @pl.when(u >= TAPS)
            def _():
                result_copy(u, False).start()

    def tick(s):
        for j in range(6, 0, -1):
            late = s - 2 - LAGS[j - 1]
            is_one = late >= BASE_ONE
            q = jnp.where(is_one, late - BASE_ONE, late)
            in_pair = lax.rem(jnp.maximum(q, 0), 3)
            v = 2 * lax.div(jnp.maximum(q, 0), 3) + in_pair

            @pl.when((q >= 0) & (in_pair < 2) & (v < TAPS))
            def _():
                stage(jnp.where(is_one, TAPS, 0) + v, j)

    def send_first(u):
        for c in unit_copies(u, 0):
            c.start()

    def tap_sum(lhs_t, plane, tap_row):
        total = None
        for q in range(CHUNKS):
            part = jnp.dot(lhs_t[:, SPAN * q:SPAN * (q + 1)], plane[pl.ds(2 - tap_row + STEP * q, STEP)].reshape(SPAN, CH), preferred_element_type=F32)
            total = part if total is None else total + part
        return total

    def shift_rows(center, minus, plus, lh, rh, first, count):
        for k in range(count):
            r = first + k
            v = center[r]
            minus[r] = jnp.concatenate([lh[pl.ds(r + 7, 1), :].astype(BF16), v[:COLS - 1]], axis=0)
            plus[r] = jnp.concatenate([v[1:], rh[pl.ds(r + 7, 1), :].astype(BF16)], axis=0)

    def conv_chunk(planes, w, i):
        total = None
        for k in range(TAPS):
            lhs = planes[k % 3][pl.ds(STEP * i + 2 - k // 3, STEP)].reshape(SPAN, CH)
            part = lax.dot_general(lhs, w[k], (((1,), (1,)), ((), ())), preferred_element_type=F32)
            total = part if total is None else total + part
        return total

    def z_chunk(i):
        z = jax.nn.gelu(av[pl.ds(STEP * i, STEP)].reshape(SPAN, CH).astype(F32), approximate=True).astype(BF16)
        zt[:, pl.ds(pl.multiple_of(SPAN * i, SPAN), SPAN)] = z.T

    def x_chunk(i):
        xt[:, pl.ds(pl.multiple_of(SPAN * i, SPAN), SPAN)] = d1[pl.ds(1 + STEP * i, STEP)].reshape(SPAN, CH).T

    def z_loop(lo, hi):
        lax.fori_loop(lo, hi, lambda i, c: (z_chunk(i), c)[1], 0)

    a_copies[0].wait()
    z_loop(0, 3)
    g_copy.wait()

    def g_edge(i, c):
        for k in range(8):
            r = 8 * i + k
            clg[pl.ds(r, 1), :] = g1[r + 1, 0:8, :].astype(F32)[0:1]
            crg[pl.ds(r, 1), :] = g1[r + 1, COLS - 8:COLS, :].astype(F32)[7:8]
        return c

    lax.fori_loop(0, ROWS // 8, g_edge, 0)
    g_frame = frame_copies(0, g1, clg, crg, lhg, rhg)
    frame_send(g_frame)
    for q in range(1, 4):
        a_copies[q].wait()
    z_loop(3, CHUNKS)

    frame_wait(g_frame)
    acc[0] = tap_sum(zt, g1, 1)
    send_first(0)

    def w2_mid(i, c):
        shift_rows(g1, g2, g0, lhg, rhg, 25 * i, 25)
        acc[1 + i] = tap_sum(zt, g1, 2 * i)
        send_first(1 + i)
        tick(1 + i)
        return c

    lax.fori_loop(0, 2, w2_mid, 0)
    x_copy.wait()
    for side, plane in ((0, g0), (1, g2)):
        def w2_side(i, c, side=side, plane=plane):
            u = 3 + 3 * side + i
            x_chunk(6 * side + 2 * i)
            x_chunk(6 * side + 2 * i + 1)
            acc[u] = tap_sum(zt, plane, i)
            send_first(u)
            tick(u)
            return c

        lax.fori_loop(0, 3, w2_side, 0)

    w2_copy.wait()
    g_planes = (g0, g1, g2)

    def da_chunk(i, dz):
        a_val = av[pl.ds(STEP * i, STEP)].reshape(SPAN, CH).astype(F32)
        d_a = (dz[...] * gelu_slope(a_val)).astype(BF16).reshape(STEP, COLS, CH)
        d1[pl.ds(1 + STEP * i, STEP)] = d_a
        for k in range(STEP):
            cld[pl.ds(STEP * i + k, 1), :] = d_a[k, 0:8].astype(F32)[0:1]
            crd[pl.ds(STEP * i + k, 1), :] = d_a[k, COLS - 8:COLS].astype(F32)[7:8]

    dza[...] = conv_chunk(g_planes, w2, 0)
    tick(TAPS)

    def dz_pair(i, c):
        dzb[...] = conv_chunk(g_planes, w2, 2 * i + 1)
        da_chunk(2 * i, dza)
        tick(TAPS + 2 * i + 1)
        dza[...] = conv_chunk(g_planes, w2, 2 * i + 2)
        da_chunk(2 * i + 1, dzb)
        tick(TAPS + 2 * i + 2)
        return c

    lax.fori_loop(0, CHUNKS // 2 - 1, dz_pair, 0)
    dzb[...] = conv_chunk(g_planes, w2, CHUNKS - 1)
    da_chunk(CHUNKS - 2, dza)
    da_chunk(CHUNKS - 1, dzb)
    tick(TAPS + CHUNKS - 1)

    d_frame = frame_copies(1, d1, cld, crd, lhd, rhd)
    frame_send(d_frame)
    acc[TAPS] = tap_sum(xt, d1, 1)
    send_first(TAPS)
    tick(BASE_ONE)
    frame_wait(d_frame)

    def w1_mid(i, c):
        shift_rows(d1, d2, d0, lhd, rhd, 25 * i, 25)
        acc[TAPS + 1 + i] = tap_sum(xt, d1, 2 * i)
        send_first(TAPS + 1 + i)
        tick(BASE_ONE + 1 + i)
        return c

    lax.fori_loop(0, 2, w1_mid, 0)
    for side, plane in ((0, d0), (1, d2)):
        def w1_side(i, c, side=side, plane=plane):
            v = 3 + 3 * side + i
            acc[TAPS + v] = tap_sum(xt, plane, i)
            send_first(TAPS + v)
            tick(BASE_ONE + v)
            return c

        lax.fori_loop(0, 3, w1_side, 0)

    w1_copy.wait()
    d_planes = (d0, d1, d2)

    def dx_copy(i):
        return pltpu.make_async_copy(av.at[pl.ds(STEP * i, STEP)], dx_hbm.at[pl.ds(STEP * i, STEP)], out_sem.at[i])

    def dx_chunk(i, c):
        total = conv_chunk(d_planes, w1, i) + g1[pl.ds(1 + STEP * i, STEP)].reshape(SPAN, CH).astype(F32)
        av[pl.ds(STEP * i, STEP)] = total.astype(BF16).reshape(STEP, COLS, CH)
        dx_copy(i).start()
        tick(BASE_ONE + TAPS + i)
        return c

    lax.fori_loop(0, CHUNKS, dx_chunk, 0)

    lax.fori_loop(LAST_TICK, BASE_ONE + 2 + 12 + LAGS[-1] + 1, lambda s, c: (tick(s), c)[1], 0)
    frame_done(g_frame)
    frame_done(d_frame)
    lax.fori_loop(0, TAPS, lambda u, c: (result_copy(u, True).wait(), c)[1], 0)
    lax.fori_loop(TAPS, 2 * TAPS, lambda u, c: (result_copy(u, False).wait(), c)[1], 0)
    lax.fori_loop(0, CHUNKS, lambda i, c: (dx_copy(i).wait(), c)[1], 0)


def solution(mesh):
    n_row, n_col = mesh.shape["row"], mesh.shape["col"]

    def local_step(x_tile, a_tile, g_tile, w_one, w_two):
        units = 2 * TAPS
        hbm = pl.BlockSpec(memory_space=pl.ANY)
        wide = pltpu.VMEM((ROWS + 2, COLS, CH), BF16)
        frame = pltpu.VMEM((64, CH), F32)
        edge = pltpu.VMEM((ROWS, CH), F32)
        d_x, d_w1, d_w2 = pl.pallas_call(
            functools.partial(kernel, n_row, n_col),
            out_shape=(
                jax.ShapeDtypeStruct((ROWS, COLS, CH), BF16),
                jax.ShapeDtypeStruct((TAPS, CH, CH), F32),
                jax.ShapeDtypeStruct((TAPS, CH, CH), F32),
            ),
            in_specs=[hbm] * 5,
            out_specs=(hbm,) * 3,
            scratch_shapes=[
                wide, wide, wide, wide, wide, wide,
                pltpu.VMEM((CH, PIX), BF16),
                pltpu.VMEM((CH, PIX), BF16),
                pltpu.VMEM((ROWS, COLS, CH), BF16),
                pltpu.VMEM((TAPS, CH, CH), BF16),
                pltpu.VMEM((TAPS, CH, CH), BF16),
                pltpu.VMEM((units, CH, CH), F32),
                pltpu.VMEM((units, CH, CH), F32),
                pltpu.VMEM((units, 128, CH), F32),
                pltpu.VMEM((units, 64, CH), F32),
                pltpu.VMEM((units, 32, CH), F32),
                pltpu.VMEM((SPAN, CH), F32),
                pltpu.VMEM((SPAN, CH), F32),
                frame, frame, frame, frame,
                edge, edge, edge, edge,
                pltpu.SemaphoreType.DMA((8,)),
                pltpu.SemaphoreType.DMA((CHUNKS,)),
                pltpu.SemaphoreType.DMA((units,)),
                pltpu.SemaphoreType.DMA((2, 5)),
                pltpu.SemaphoreType.DMA((2, 5)),
                pltpu.SemaphoreType.DMA((units, 10)),
                pltpu.SemaphoreType.DMA((units, 10)),
            ],
            compiler_params=pltpu.CompilerParams(collective_id=0, has_side_effects=True, vmem_limit_bytes=67043328),
        )(x_tile[0], a_tile[0], g_tile[0], w_one.reshape(TAPS, CH, CH), w_two.reshape(TAPS, CH, CH))
        shape = (3, 3, CH, CH)
        return d_x[None], d_w1.reshape(shape), d_w2.reshape(shape)

    tile_spec = P(None, "row", "col", None)
    return jax.shard_map(local_step, mesh=mesh, in_specs=(tile_spec, tile_spec, tile_spec, P(), P()), out_specs=(tile_spec, P(), P()), check_vma=False)
```

time: 245 us -> 114 us (0.47); the launches traced: 241 us -> 114 us
  Pallas kernels: 0 us -> 105 us
  matrix products: 89.1 us -> 0 us
  waiting for transfers between devices: 39.5 us -> 0 us
  other arithmetic: 36.8 us -> 0 us
  local copies, waits for them, and re-layouts: 38.6 us -> 9.13 us
  starting transfers between devices: 22 us -> 0 us
  between operations: 14.9 us -> 0.65 us
    pallas_call x0 -> x1, Pallas kernels: none -> 105 us  [local_step(): pl.pallas_call(functools.partial(kernel, n_row, n_col), out_shape=(jax.Sh...]
    dot_general x18 -> x0, matrix products: 57.7 us -> none  [tap_grads(): jnp.einsum('bhwi,bhwo->io', tile_in, grad_wide[:, 2 - tap_row:2 - tap_row...]
    psum x1 -> x0, waiting for transfers between devices: 37.9 us -> none  [local_step(): d_w1, d_w2 = lax.psum((w1_part, w2_part), ('row', 'col'))]
    conv_general_dilated x2 -> x0, matrix products: 31.3 us -> none  [conv_valid(): lax.conv_general_dilated(lhs_arr, rhs_arr, (1, 1), 'VALID', dimension_num...]
    ppermute x8 -> x0, starting transfers between devices: 21.9 us -> none  [the longest x2 9.85 us: add_halo(): from_left = lax.ppermute(tall[:, :, -1:], 'col', col_down)]
    conv_general_dilated x7 -> x0, local copies, waits for them, and re-layouts: 20.7 us -> none  [conv_valid(): lax.conv_general_dilated(lhs_arr, rhs_arr, (1, 1), 'VALID', dimension_num...]
    convert_element_type x2 -> x0, other arithmetic: 19.6 us -> none  [the longest x1 11.6 us: local_step(): d_a = (d_z * gelu_slope(a_val)).astype(jnp.bfloat16)]
    concatenate x3 -> x0, other arithmetic: 13.5 us -> none  [add_halo(): return jnp.concatenate([from_left, tall, from_right], axis=2)]
  transfers between devices with their start and end apart: 9 -> 0, of which waited for: 2 -> 0; matrix products, arithmetic and copies ran while one was open for 37% -> 0% of each run, Pallas kernels for 0% -> 0%
where the time goes in v1:
time: 114 us
  Pallas kernels  105 us (92%)
  local copies, waits for them, and re-layouts  9.13 us (8%)
    pallas_call x1, Pallas kernels, local_step(): pl.pallas_call(functools.partial(kernel, n_row, n_col), out_shape=(jax.Sh...  105 us
    unnamed x7, local copies, waits for them, and re-layouts  9.13 us

profile of v1, /device:TPU:0, one launch (start us, length us, event | category | flops | bytes accessed | tf_op | source)
XLA Modules:
  0.0 114.3 jit_solution(12156845807091077109)
XLA Ops:
  0.6 104.6 %shard_map.76 = (bf16[48,192,256]{2,1,0:T(8,128)(2,1)}, f32[9,256,256]{2,1,0:T(8,128)}, f32[9,256,256]{2,1,0:T(8,128)}) custom-call(bf16[48,192,256]{2,1,0:T(8,128)(2,1)} %bitcast.9, bf16[48,192,256]{2,1,0:T(8,128)(2,1)} %bitcast.10, bf16[48,192,256]{2,1,0:T(8,128)(2,1)} %bitcast.11, bf16[9,256,256]{2,1,0:T(8,128)(2,1)} %bitcast.14, ...), custom_call_target="tpu_custom_call" | custom-call | tf_op jit(solution)/shard_map/pallas_call | solution.py:374
  105.2 0.0 copy-start.1
  105.2 5.2 %copy.11 = bf16[1,48,192,256]{3,2,1,0:T(8,128)(2,1)} copy(bf16[1,48,192,256]{3,2,1,0:T(8,128)(2,1)} %bitcast.8) | data formatting | bytes 9437184
  110.4 0.0 copy-done.1
  110.4 0.0 copy-start
  110.4 1.4 %copy.12 = f32[3,3,256,256]{3,2,1,0:T(8,128)} copy(f32[3,3,256,256]{3,2,1,0:T(8,128)S(1)} %bitcast.13) | data formatting | bytes 4718592
  111.8 1.1 copy-done
  112.9 1.4 %copy.13 = f32[3,3,256,256]{3,2,1,0:T(8,128)} copy(f32[3,3,256,256]{3,2,1,0:T(8,128)S(1)} %bitcast.12) | data formatting | bytes 4718592
Async XLA Ops:
  105.2 5.2 %copy-start.1 = (f32[9,256,256]{2,1,0:T(8,128)S(1)}, f32[9,256,256]{2,1,0:T(8,128)}, u32[]{:S(2)}) copy-start(f32[9,256,256]{2,1,0:T(8,128)} %get-tuple-element.7) | copy-start | bytes 7077892
  110.4 2.5 %copy-start = (f32[9,256,256]{2,1,0:T(8,128)S(1)}, f32[9,256,256]{2,1,0:T(8,128)}, u32[]{:S(2)}) copy-start(f32[9,256,256]{2,1,0:T(8,128)} %get-tuple-element.8) | copy-start | bytes 7077892

commit v2 on v1

--- a/solution.py
+++ b/solution.py
@@ -18,27 +18,48 @@
 SPAN = STEP * COLS
 CHUNKS = ROWS // STEP
 TAPS = 9
-BASE_ONE = TAPS + CHUNKS
-LAST_TICK = 2 * (TAPS + CHUNKS)
-LAGS = (0, 2, 4, 6, 8, 10)
-
-
-def gelu_slope(pre_act):
-    tanh_scale = 0.7978845608028654
-    cube_coef = 0.044715
-    tanh_val = jnp.tanh(tanh_scale * (pre_act + cube_coef * pre_act * pre_act * pre_act))
-    return 0.5 * (1.0 + tanh_val) + 0.5 * pre_act * (1.0 - tanh_val * tanh_val) * tanh_scale * (1.0 + 3.0 * cube_coef * pre_act * pre_act)
+TAP_ORDER = ((1, 1), (0, 1), (2, 1), (0, 0), (1, 0), (2, 0), (0, 2), (1, 2), (2, 2))
+DZ_PLAN = (
+    ((1, 8), (2, 6), (3, 3), (4, 0)),
+    ((2, 7), (3, 4), (4, 1), (4, 2)),
+    ((2, 8), (3, 5), (3, 6), (4, 3), (5, 0)),
+    ((3, 7), (4, 4), (4, 5), (5, 1), (5, 2)),
+    ((3, 8), (4, 6), (5, 3), (6, 0)),
+    ((4, 7), (5, 4), (5, 5), (6, 1)),
+)
+W1_PLAN = (
+    ((4, 8), (5, 6), (6, 2)),
+    ((1, 9), (5, 7), (6, 3), (6, 4)),
+    ((1, 10), (5, 8), (6, 5), (6, 6)),
+)
+DX_PLAN = (
+    ((1, 17), (2, 15), (3, 12), (4, 9), (4, 10), (6, 7)),
+    ((2, 16), (3, 13), (3, 14), (4, 11), (5, 9), (5, 10), (6, 8)),
+    ((2, 17), (3, 15), (4, 12), (4, 13), (5, 11), (6, 9)),
+    ((3, 16), (3, 17), (4, 14), (4, 15), (5, 12), (5, 13), (6, 10)),
+    ((4, 16), (4, 17), (5, 14), (5, 15), (6, 11), (6, 12)),
+    ((5, 16), (5, 17), (6, 13), (6, 14)),
+    ((6, 15), (6, 16), (6, 17)),
+)
+
+
+def gelu_slope(a):
+    scale = 0.7978845608028654
+    square = (scale * 0.044715 * a) * a
+    tanh_val = jnp.tanh(a * (scale + square))
+    return (0.5 + 0.5 * tanh_val) + (0.5 * a * (1.0 - tanh_val * tanh_val)) * (scale + 3.0 * square)
 
 
 def kernel(n_row, n_col, x_hbm, a_hbm, g_hbm, w1_hbm, w2_hbm, dx_hbm, dw1_hbm, dw2_hbm,
-           g0, g1, g2, d0, d1, d2, zt, xt, av, w1, w2, acc, res, r0, r1, r2, dza, dzb,
+           planes, zt, xt, av, w1, w2, acc, res, r0, r1, r2, dza, dzb,
            lhg, rhg, lhd, rhd, clg, crg, cld, crd,
            in_sem, out_sem, dw_sem, hs_sem, hr_sem, as_sem, ar_sem):
     row = lax.axis_index("row")
     col = lax.axis_index("col")
-    bx = lax.rem(col, 2)
-    by = lax.div(col, 2)
+    by = jnp.where(col >= 2, 1, 0)
+    bx = col - 2 * by
     other = 1 - row
+    g0, g1, g2, d0, d1, d2 = (planes.at[k] for k in range(6))
     col_x = col + 1 - 2 * bx
     col_y = col + 2 - 4 * by
     has_left = col > 0
@@ -156,15 +177,10 @@
         at = pl.ds(pl.multiple_of(start, 16), size)
         dst[u, at, :] = acc[u, at, :] + src[u, pl.ds(src_start, size), :]
 
-    def tap_of(v):
-        tap_row = jnp.where(v < 1, 1, jnp.where(v < 3, 2 * (v - 1), lax.rem(v, 3)))
-        tap_col = jnp.where(v < 3, 1, jnp.where(v < 6, 0, 2))
-        return 3 * tap_row + tap_col
-
-    def result_copy(u, first):
-        if first:
-            return pltpu.make_async_copy(res.at[u], dw2_hbm.at[tap_of(u)], dw_sem.at[u])
-        return pltpu.make_async_copy(res.at[u], dw1_hbm.at[tap_of(u - TAPS)], dw_sem.at[u])
+    def result_copy(u):
+        out = dw2_hbm if u < TAPS else dw1_hbm
+        tap_row, tap_col = TAP_ORDER[u % TAPS]
+        return pltpu.make_async_copy(res.at[u], out.at[3 * tap_row + tap_col], dw_sem.at[u])
 
     def stage(u, j):
         for c in unit_copies(u, j - 1):
@@ -186,58 +202,60 @@
                 for c in unit_copies(u, k):
                     c.wait_send()
 
-            @pl.when(u < TAPS)
-            def _():
-                result_copy(u, True).start()
-
-            @pl.when(u >= TAPS)
-            def _():
-                result_copy(u, False).start()
-
-    def tick(s):
-        for j in range(6, 0, -1):
-            late = s - 2 - LAGS[j - 1]
-            is_one = late >= BASE_ONE
-            q = jnp.where(is_one, late - BASE_ONE, late)
-            in_pair = lax.rem(jnp.maximum(q, 0), 3)
-            v = 2 * lax.div(jnp.maximum(q, 0), 3) + in_pair
-
-            @pl.when((q >= 0) & (in_pair < 2) & (v < TAPS))
-            def _():
-                stage(jnp.where(is_one, TAPS, 0) + v, j)
+            result_copy(u).start()
+
+    def run(plan):
+        for j, u in plan:
+            stage(u, j)
 
     def send_first(u):
         for c in unit_copies(u, 0):
             c.start()
 
-    def tap_sum(lhs_t, plane, tap_row):
+    def tap_sum(lhs_t, plane, tap_row, fill=()):
         total = None
+        blocks = SPAN // CH
         for q in range(CHUNKS):
-            part = jnp.dot(lhs_t[:, SPAN * q:SPAN * (q + 1)], plane[pl.ds(2 - tap_row + STEP * q, STEP)].reshape(SPAN, CH), preferred_element_type=F32)
-            total = part if total is None else total + part
+            rhs = plane[pl.ds(2 - tap_row + STEP * q, STEP)].reshape(SPAN, CH)
+            for m in range(blocks):
+                for piece in fill[blocks * q + m::CHUNKS * blocks]:
+                    piece()
+                part = jnp.dot(lhs_t[blocks * q + m], rhs[CH * m:CH * (m + 1)], preferred_element_type=F32)
+                total = part if total is None else total + part
         return total
 
-    def shift_rows(center, minus, plus, lh, rh, first, count):
-        for k in range(count):
-            r = first + k
-            v = center[r]
-            minus[r] = jnp.concatenate([lh[pl.ds(r + 7, 1), :].astype(BF16), v[:COLS - 1]], axis=0)
-            plus[r] = jnp.concatenate([v[1:], rh[pl.ds(r + 7, 1), :].astype(BF16)], axis=0)
-
-    def conv_chunk(planes, w, i):
-        total = None
+    def shift_row(center, minus, plus, r, lh=None, rh=None):
+        v = center[r]
+        first = v[:1] if lh is None else lh[pl.ds(r + 7, 1), :].astype(BF16)
+        last = v[:1] if rh is None else rh[pl.ds(r + 7, 1), :].astype(BF16)
+        minus[r] = jnp.concatenate([first, v[:COLS - 1]], axis=0)
+        plus[r] = jnp.concatenate([v[1:], last], axis=0)
+
+    def mend_row(minus, plus, r, lh, rh):
+        at = lax.broadcasted_iota(jnp.int32, (8, CH), 0)
+        minus[r, 0:8] = jnp.where(at == 0, lh[pl.ds(r + 7, 1), :], minus[r, 0:8].astype(F32)).astype(BF16)
+        plus[r, COLS - 8:COLS] = jnp.where(at == 7, rh[pl.ds(r + 7, 1), :], plus[r, COLS - 8:COLS].astype(F32)).astype(BF16)
+
+    def conv_pair(planes, w, i, fill=()):
+        totals = [None, None]
         for k in range(TAPS):
-            lhs = planes[k % 3][pl.ds(STEP * i + 2 - k // 3, STEP)].reshape(SPAN, CH)
-            part = lax.dot_general(lhs, w[k], (((1,), (1,)), ((), ())), preferred_element_type=F32)
-            total = part if total is None else total + part
-        return total
+            for n in range(2):
+                lhs = planes[k % 3][pl.ds(STEP * (2 * i + n) + 2 - k // 3, STEP)].reshape(SPAN, CH)
+                part = lax.dot_general(lhs, w[k], (((1,), (1,)), ((), ())), preferred_element_type=F32)
+                totals[n] = part if k == 0 else totals[n] + part
+            for piece in fill[len(fill) * k // TAPS:len(fill) * (k + 1) // TAPS]:
+                piece()
+        return totals
 
     def z_chunk(i):
         z = jax.nn.gelu(av[pl.ds(STEP * i, STEP)].reshape(SPAN, CH).astype(F32), approximate=True).astype(BF16)
-        zt[:, pl.ds(pl.multiple_of(SPAN * i, SPAN), SPAN)] = z.T
+        for m in range(SPAN // CH):
+            zt[SPAN // CH * i + m] = z[CH * m:CH * (m + 1)].T
 
     def x_chunk(i):
-        xt[:, pl.ds(pl.multiple_of(SPAN * i, SPAN), SPAN)] = d1[pl.ds(1 + STEP * i, STEP)].reshape(SPAN, CH).T
+        x = d1[pl.ds(1 + STEP * i, STEP)].reshape(SPAN, CH)
+        for m in range(SPAN // CH):
+            xt[SPAN // CH * i + m] = x[CH * m:CH * (m + 1)].T
 
     def z_loop(lo, hi):
         lax.fori_loop(lo, hi, lambda i, c: (z_chunk(i), c)[1], 0)
@@ -260,106 +278,140 @@
         a_copies[q].wait()
     z_loop(3, CHUNKS)
 
-    frame_wait(g_frame)
     acc[0] = tap_sum(zt, g1, 1)
     send_first(0)
+    frame_wait(g_frame)
 
     def w2_mid(i, c):
-        shift_rows(g1, g2, g0, lhg, rhg, 25 * i, 25)
-        acc[1 + i] = tap_sum(zt, g1, 2 * i)
+        acc[1 + i] = tap_sum(zt, g1, 2 * i, [functools.partial(shift_row, g1, g2, g0, 25 * i + k, lhg, rhg) for k in range(25)])
         send_first(1 + i)
-        tick(1 + i)
+        stage(i, 1)
         return c
 
     lax.fori_loop(0, 2, w2_mid, 0)
     x_copy.wait()
-    for side, plane in ((0, g0), (1, g2)):
-        def w2_side(i, c, side=side, plane=plane):
-            u = 3 + 3 * side + i
-            x_chunk(6 * side + 2 * i)
-            x_chunk(6 * side + 2 * i + 1)
-            acc[u] = tap_sum(zt, plane, i)
-            send_first(u)
-            tick(u)
-            return c
-
-        lax.fori_loop(0, 3, w2_side, 0)
+
+    def w2_left(i, c):
+        x_chunk(2 * i)
+        x_chunk(2 * i + 1)
+        acc[3 + i] = tap_sum(zt, g0, i)
+        send_first(3 + i)
+        stage(2 + i, 1)
+        stage(i, 2)
+        return c
+
+    def w2_right(i, c):
+        x_chunk(6 + 2 * i)
+        x_chunk(6 + 2 * i + 1)
+        acc[6 + i] = tap_sum(zt, g2, i)
+        send_first(6 + i)
+        stage(5 + i, 1)
+        stage(3 + i, 2)
+        stage(i, 3)
+        return c
+
+    lax.fori_loop(0, 3, w2_left, 0)
+    lax.fori_loop(0, 3, w2_right, 0)
 
     w2_copy.wait()
     g_planes = (g0, g1, g2)
 
     def da_chunk(i, dz):
-        a_val = av[pl.ds(STEP * i, STEP)].reshape(SPAN, CH).astype(F32)
-        d_a = (dz[...] * gelu_slope(a_val)).astype(BF16).reshape(STEP, COLS, CH)
-        d1[pl.ds(1 + STEP * i, STEP)] = d_a
+        part = COLS // 3
+
+        def one(k, third):
+            r, at = STEP * i + k, part * third
+            a_val = av[r, at:at + part].astype(F32)
+            d_a = (dz[COLS * k + at:COLS * k + at + part] * gelu_slope(a_val)).astype(BF16)
+            d1[1 + r, at:at + part] = d_a
+            if third == 0:
+                cld[pl.ds(r, 1), :] = d_a[0:8].astype(F32)[0:1]
+            if third == 2:
+                crd[pl.ds(r, 1), :] = d_a[part - 8:].astype(F32)[7:8]
+
+        pieces = []
         for k in range(STEP):
-            cld[pl.ds(STEP * i + k, 1), :] = d_a[k, 0:8].astype(F32)[0:1]
-            crd[pl.ds(STEP * i + k, 1), :] = d_a[k, COLS - 8:COLS].astype(F32)[7:8]
-
-    dza[...] = conv_chunk(g_planes, w2, 0)
-    tick(TAPS)
-
-    def dz_pair(i, c):
-        dzb[...] = conv_chunk(g_planes, w2, 2 * i + 1)
-        da_chunk(2 * i, dza)
-        tick(TAPS + 2 * i + 1)
-        dza[...] = conv_chunk(g_planes, w2, 2 * i + 2)
-        da_chunk(2 * i + 1, dzb)
-        tick(TAPS + 2 * i + 2)
-        return c
-
-    lax.fori_loop(0, CHUNKS // 2 - 1, dz_pair, 0)
-    dzb[...] = conv_chunk(g_planes, w2, CHUNKS - 1)
-    da_chunk(CHUNKS - 2, dza)
-    da_chunk(CHUNKS - 1, dzb)
-    tick(TAPS + CHUNKS - 1)
+            pieces += [functools.partial(one, k, third) for third in range(3)]
+            pieces.append(functools.partial(shift_row, d1, d2, d0, 1 + STEP * i + k))
+        return pieces
+
+    def dz_store(pair):
+        dza[...], dzb[...] = pair
+
+    def run_at(i, plans):
+        for k, plan in enumerate(plans):
+            @pl.when(i == k)
+            def _(plan=plan):
+                run(plan)
+
+    def dz_step(i, c):
+        dz_store(conv_pair(g_planes, w2, i, da_chunk(2 * i - 2, dza) + da_chunk(2 * i - 1, dzb)))
+        run_at(i - 1, DZ_PLAN[1:])
+        return c
+
+    dz_store(conv_pair(g_planes, w2, 0))
+    run(DZ_PLAN[0])
+    lax.fori_loop(1, CHUNKS // 2, dz_step, 0)
 
     d_frame = frame_copies(1, d1, cld, crd, lhd, rhd)
+    acc[9] = tap_sum(xt, d1, 1, da_chunk(CHUNKS - 2, dza) + da_chunk(CHUNKS - 1, dzb))
     frame_send(d_frame)
-    acc[TAPS] = tap_sum(xt, d1, 1)
-    send_first(TAPS)
-    tick(BASE_ONE)
+    send_first(9)
+    run(W1_PLAN[0])
     frame_wait(d_frame)
+    shift_row(d1, d2, d0, 0)
+    shift_row(d1, d2, d0, ROWS + 1)
 
     def w1_mid(i, c):
-        shift_rows(d1, d2, d0, lhd, rhd, 25 * i, 25)
-        acc[TAPS + 1 + i] = tap_sum(xt, d1, 2 * i)
-        send_first(TAPS + 1 + i)
-        tick(BASE_ONE + 1 + i)
+        acc[10 + i] = tap_sum(xt, d1, 2 * i, [functools.partial(mend_row, d2, d0, 25 * i + k, lhd, rhd) for k in range(25)])
+        send_first(10 + i)
+        run_at(i, W1_PLAN[1:])
         return c
 
     lax.fori_loop(0, 2, w1_mid, 0)
-    for side, plane in ((0, d0), (1, d2)):
-        def w1_side(i, c, side=side, plane=plane):
-            v = 3 + 3 * side + i
-            acc[TAPS + v] = tap_sum(xt, plane, i)
-            send_first(TAPS + v)
-            tick(BASE_ONE + v)
-            return c
-
-        lax.fori_loop(0, 3, w1_side, 0)
+
+    def w1_left(i, c):
+        acc[12 + i] = tap_sum(xt, d0, i)
+        send_first(12 + i)
+        stage(11 + i, 1)
+        stage(9 + i, 2)
+        return c
+
+    def w1_right(i, c):
+        acc[15 + i] = tap_sum(xt, d2, i)
+        send_first(15 + i)
+        stage(14 + i, 1)
+        stage(12 + i, 2)
+        stage(9 + i, 3)
+        return c
+
+    lax.fori_loop(0, 3, w1_left, 0)
+    lax.fori_loop(0, 3, w1_right, 0)
 
     w1_copy.wait()
     d_planes = (d0, d1, d2)
 
     def dx_copy(i):
-        return pltpu.make_async_copy(av.at[pl.ds(STEP * i, STEP)], dx_hbm.at[pl.ds(STEP * i, STEP)], out_sem.at[i])
-
-    def dx_chunk(i, c):
-        total = conv_chunk(d_planes, w1, i) + g1[pl.ds(1 + STEP * i, STEP)].reshape(SPAN, CH).astype(F32)
-        av[pl.ds(STEP * i, STEP)] = total.astype(BF16).reshape(STEP, COLS, CH)
+        at = pl.ds(2 * STEP * i, 2 * STEP)
+        return pltpu.make_async_copy(av.at[at], dx_hbm.at[at], out_sem.at[i])
+
+    def dx_step(i, c):
+        for n, total in enumerate(conv_pair(d_planes, w1, i)):
+            at = STEP * (2 * i + n)
+            total = total + g1[pl.ds(1 + at, STEP)].reshape(SPAN, CH).astype(F32)
+            av[pl.ds(at, STEP)] = total.astype(BF16).reshape(STEP, COLS, CH)
         dx_copy(i).start()
-        tick(BASE_ONE + TAPS + i)
-        return c
-
-    lax.fori_loop(0, CHUNKS, dx_chunk, 0)
-
-    lax.fori_loop(LAST_TICK, BASE_ONE + 2 + 12 + LAGS[-1] + 1, lambda s, c: (tick(s), c)[1], 0)
+        run_at(i, DX_PLAN[:CHUNKS // 2])
+        return c
+
+    lax.fori_loop(0, CHUNKS // 2, dx_step, 0)
+    run(DX_PLAN[CHUNKS // 2])
+
     frame_done(g_frame)
     frame_done(d_frame)
-    lax.fori_loop(0, TAPS, lambda u, c: (result_copy(u, True).wait(), c)[1], 0)
-    lax.fori_loop(TAPS, 2 * TAPS, lambda u, c: (result_copy(u, False).wait(), c)[1], 0)
-    lax.fori_loop(0, CHUNKS, lambda i, c: (dx_copy(i).wait(), c)[1], 0)
+    for u in range(2 * TAPS):
+        result_copy(u).wait()
+    lax.fori_loop(0, CHUNKS // 2, lambda i, c: (dx_copy(i).wait(), c)[1], 0)
 
 
 def solution(mesh):
@@ -368,7 +420,6 @@
     def local_step(x_tile, a_tile, g_tile, w_one, w_two):
         units = 2 * TAPS
         hbm = pl.BlockSpec(memory_space=pl.ANY)
-        wide = pltpu.VMEM((ROWS + 2, COLS, CH), BF16)
         frame = pltpu.VMEM((64, CH), F32)
         edge = pltpu.VMEM((ROWS, CH), F32)
         d_x, d_w1, d_w2 = pl.pallas_call(
@@ -381,9 +432,9 @@
             in_specs=[hbm] * 5,
             out_specs=(hbm,) * 3,
             scratch_shapes=[
-                wide, wide, wide, wide, wide, wide,
-                pltpu.VMEM((CH, PIX), BF16),
-                pltpu.VMEM((CH, PIX), BF16),
+                pltpu.VMEM((6, ROWS + 2, COLS, CH), BF16),
+                pltpu.VMEM((PIX // CH, CH, CH), BF16),
+                pltpu.VMEM((PIX // CH, CH, CH), BF16),
                 pltpu.VMEM((ROWS, COLS, CH), BF16),
                 pltpu.VMEM((TAPS, CH, CH), BF16),
                 pltpu.VMEM((TAPS, CH, CH), BF16),
@@ -397,7 +448,7 @@
                 frame, frame, frame, frame,
                 edge, edge, edge, edge,
                 pltpu.SemaphoreType.DMA((8,)),
-                pltpu.SemaphoreType.DMA((CHUNKS,)),
+                pltpu.SemaphoreType.DMA((CHUNKS // 2,)),
                 pltpu.SemaphoreType.DMA((units,)),
                 pltpu.SemaphoreType.DMA((2, 5)),
                 pltpu.SemaphoreType.DMA((2, 5)),

time: 114 us -> 93.7 us (0.82)
  Pallas kernels: 105 us -> 83.8 us
    pallas_call x1, Pallas kernels: 105 us -> 83.8 us  [local_step(): pl.pallas_call(functools.partial(kernel, n_row, n_col), out_shape=(jax.Sh...]
where the time goes in v2:
time: 93.7 us; the launch traced here: 93.5 us
  Pallas kernels  83.8 us (89%)
  local copies, waits for them, and re-layouts  9.13 us (10%)
    pallas_call x1, Pallas kernels, local_step(): pl.pallas_call(functools.partial(kernel, n_row, n_col), out_shape=(jax.Sh...  83.8 us
    unnamed x7, local copies, waits for them, and re-layouts  9.13 us

profile of v2, /device:TPU:0, one launch (start us, length us, event | category | flops | bytes accessed | tf_op | source)
XLA Modules:
  0.0 93.5 jit_solution(2638786269819386571)
XLA Ops:
  0.6 83.8 %shard_map.76 = (bf16[48,192,256]{2,1,0:T(8,128)(2,1)}, f32[9,256,256]{2,1,0:T(8,128)}, f32[9,256,256]{2,1,0:T(8,128)}) custom-call(bf16[48,192,256]{2,1,0:T(8,128)(2,1)} %bitcast.9, bf16[48,192,256]{2,1,0:T(8,128)(2,1)} %bitcast.10, bf16[48,192,256]{2,1,0:T(8,128)(2,1)} %bitcast.11, bf16[9,256,256]{2,1,0:T(8,128)(2,1)} %bitcast.14, ...), custom_call_target="tpu_custom_call" | custom-call | tf_op jit(solution)/shard_map/pallas_call | solution.py:425
  84.4 0.0 copy-start.1
  84.4 5.2 %copy.11 = bf16[1,48,192,256]{3,2,1,0:T(8,128)(2,1)} copy(bf16[1,48,192,256]{3,2,1,0:T(8,128)(2,1)} %bitcast.8) | data formatting | bytes 9437184
  89.6 0.0 copy-done.1
  89.6 0.0 copy-start
  89.6 1.4 %copy.12 = f32[3,3,256,256]{3,2,1,0:T(8,128)} copy(f32[3,3,256,256]{3,2,1,0:T(8,128)S(1)} %bitcast.13) | data formatting | bytes 4718592
  91.0 1.1 %copy-done = f32[9,256,256]{2,1,0:T(8,128)S(1)} copy-done((f32[9,256,256]{2,1,0:T(8,128)S(1)}, f32[9,256,256]{2,1,0:T(8,128)}, u32[]{:S(2)}) %copy-start) | copy-done | bytes 2359320
  92.1 1.4 %copy.13 = f32[3,3,256,256]{3,2,1,0:T(8,128)} copy(f32[3,3,256,256]{3,2,1,0:T(8,128)S(1)} %bitcast.12) | data formatting | bytes 4718592
Async XLA Ops:
  84.4 5.2 %copy-start.1 = (f32[9,256,256]{2,1,0:T(8,128)S(1)}, f32[9,256,256]{2,1,0:T(8,128)}, u32[]{:S(2)}) copy-start(f32[9,256,256]{2,1,0:T(8,128)} %get-tuple-element.7) | copy-start | bytes 7077892
  89.6 2.5 %copy-start = (f32[9,256,256]{2,1,0:T(8,128)S(1)}, f32[9,256,256]{2,1,0:T(8,128)}, u32[]{:S(2)}) copy-start(f32[9,256,256]{2,1,0:T(8,128)} %get-tuple-element.8) | copy-start | bytes 7077892
